TPU v7x, 32 devices: a whole 2x2x4 slice. The times are simulated.
32 devices in a mesh: pix: 8 (over z, x), band: 4 (over y, core).
Axes of the slice: x: 2, y: 2, z: 4, core: 2. Of those that a mesh axis runs over, the one named last changes fastest.
Arguments:
- spectra: bfloat16 [224, 32768], P('band', 'pix'), may hold values from -0.1 to 4
- endmembers: bfloat16 [224, 512], P('band'), may hold values from 0.05 to 1
- gram_inverse: float32 [512, 512], replicated, may hold values from -1 to 1, as said below
- abundances: float32 [512, 32768], P(None, ('pix', 'band')), may hold values from 0 to 512, as said below
- duals: float32 [512, 32768], P(None, ('pix', 'band')), may hold values from -4 to 4
Outputs:
- abundances_out: float32 [512, 32768], P(None, ('pix', 'band'))
- duals_out: float32 [512, 32768], P(None, ('pix', 'band'))
- residual_rms: float32 [2, 2], replicated
Inputs may be any that keep to these rules, and one draw needn't show every extreme that they name: `abundances`: each column is nonnegative and sums to 512. `gram_inverse`: penalty times the float32 inverse of endmembers^T endmembers / 512^2 + penalty I, with penalty = 224 / (2 * 512^2) and the endmembers as stored.
All inputs are finite; a program needn't handle non-finite values.
Results may differ from a plain program's by a relative error of at most 0.0004.
Values may be sent and summed in bfloat16 or wider, within the bound.
No kernel may reach another device: no remote copies, remote signals or barrier semaphores. Data moves between devices by JAX's collectives and lax.ppermute only.
A program may use at most 64 MiB of HBM per device.

v0:
```python
import jax
import jax.numpy as jnp
from jax import lax
from jax.sharding import PartitionSpec as P

B = 224
K = 512
ITERS = 2
BISECT = 6


def project(shifted):
    simplex_sum = float(K)
    high_end = jnp.max(shifted, axis=0)
    low_end = (jnp.sum(shifted, axis=0) - simplex_sum) / simplex_sum

    def mass_at(level):
        return jnp.sum(jnp.maximum(shifted - level[None, :], 0.0), axis=0)

    mass_low = mass_at(low_end)
    mass_high = jnp.zeros_like(high_end)

    def bisect_once(unused, state):
        low_now, high_now, low_mass, high_mass = state
        middle = 0.5 * (low_now + high_now)
        total_mass = mass_at(middle)
        too_high = total_mass > simplex_sum
        return (
            jnp.where(too_high, middle, low_now),
            jnp.where(too_high, high_now, middle),
            jnp.where(too_high, total_mass, low_mass),
            jnp.where(too_high, high_mass, total_mass),
        )

    low_end, high_end, mass_low, mass_high = lax.fori_loop(
        0, BISECT, bisect_once, (low_end, high_end, mass_low, mass_high)
    )
    level = low_end + (mass_low - simplex_sum) * (high_end - low_end) / (mass_low - mass_high)
    return jnp.maximum(shifted - level[None, :], 0.0)


def contract_bands(signatures, columns):
    return lax.dot_general(
        signatures, columns, (((0,), (0,)), ((), ())), preferred_element_type=jnp.float32
    )


def body(spectra, endmembers, gram_inverse, abundances, duals):
    penalty = B / (2.0 * K * K)
    exchanged = lax.all_to_all(spectra, "band", split_axis=1, concat_axis=0, tiled=True)
    all_rows = lax.all_gather(endmembers, "band", axis=0, tiled=True)
    fit_term = contract_bands(all_rows, exchanged)
    fit_term = fit_term / K
    pixel_count = abundances.shape[1] * lax.axis_size("pix") * lax.axis_size("band")
    current = abundances
    scaled_dual = duals
    primal_list = []
    change_list = []
    for sweep in range(ITERS):
        primal = jnp.dot(
            gram_inverse,
            fit_term / penalty + current - scaled_dual,
            precision=lax.Precision.HIGHEST,
        )
        updated = project(primal + scaled_dual)
        scaled_dual = scaled_dual + primal - updated
        primal_sum = jnp.sum((primal - updated) ** 2)
        change_sum = jnp.sum((updated - current) ** 2)
        primal_sum, change_sum = lax.psum((primal_sum, change_sum), ("pix", "band"))
        primal_list.append(primal_sum)
        change_list.append(change_sum)
        current = updated
    totals = jnp.stack([jnp.stack(primal_list), jnp.stack(change_list)])
    residual_rms = jnp.sqrt(totals / pixel_count)
    return (current, scaled_dual, residual_rms)


def solution(mesh):
    return jax.shard_map(
        body,
        mesh=mesh,
        in_specs=(
            P("band", "pix"),
            P("band", None),
            P(),
            P(None, ("pix", "band")),
            P(None, ("pix", "band")),
        ),
        out_specs=(P(None, ("pix", "band")), P(None, ("pix", "band")), P()),
        check_vma=False,
    )
```

profile of v0, /device:TPU:0, one launch (start us, length us, event | category | flops | bytes accessed | tf_op | source)
XLA Modules:
  0.0 99.4 jit_solution(1292467306230520806)
XLA Ops:
  0.6 1.9 %copy.12 = bf16[7,4,8,1024]{3,2,0,1:T(8,128)(2,1)} copy(bf16[7,4,8,1024]{3,2,1,0:T(8,128)(2,1)} %bitcast.36) | data formatting | bytes 917504 | tf_op jit(solution)/shard_map/all_to_all | solution.py:50
  2.5 4.3 %all-to-all-start = ((bf16[56,4,1024]{2,0,1:T(8,128)(2,1)}), bf16[56,4,1024]{2,0,1:T(8,128)(2,1)S(1)}, u32[]{:S(2)}, u32[]{:S(2)}) async-start(bf16[56,4,1024]{2,0,1:T(8,128)(2,1)} %bitcast.34), calls=%async_computation | async-start | bytes 917504 | tf_op jit(solution)/shard_map/all_to_all | solution.py:50
  6.8 10.2 %all_gather.3 = bf16[224,512]{1,0:T(8,128)(2,1)S(1)} all-gather(bf16[56,512]{1,0:T(8,128)(2,1)} %param.10), channel_id=1, replica_groups=mesh['pix'=8,'band'=4] {'band'}, dimensions={0}, use_global_device_ids=true | all-gather | bytes 286720 | tf_op jit(solution)/shard_map/all_gather | solution.py:51
  17.0 0.5 fusion.30
  17.5 8.7 %fusion.29 = (f32[1024]{0:T(1024)S(1)}, f32[512,1024]{1,0:T(8,128)S(1)}, f32[1024,512]{0,1:T(8,128)}) fusion(f32[512,1024]{1,0:T(8,128)} %param.13, f32[512,512]{1,0:T(8,128)S(1)} %copy-done, f32[512,1024]{1,0:T(8,128)} %param.12, f32[512,1024]{1,0:T(8,128)S(1)} %fusion.30), kind=kOutput, calls=%fused_computation.54 | convolution fusion | flops 3223845888 | bytes 11538432 | tf_op jit(solution)/shard_map/dot_general | solution.py:60
  26.2 0.3 maximum_reduce_fusion.3
  26.5 1.9 %while.34 = (s32[]{:T(128)}, f32[1024]{0:T(1024)S(1)}, f32[1024]{0:T(1024)S(1)}, f32[1024]{0:T(1024)S(1)}, f32[1024]{0:T(1024)S(1)}, /*index=5*/f32[512,1024]{1,0:T(8,128)S(1)}, s32[]{:T(128)}, s32[]{:T(128)}) while((s32[]{:T(128)}, f32[1024]{0:T(1024)S(1)}, f32[1024]{0:T(1024)S(1)}, f32[1024]{0:T(1024)S(1)}, f32[1024]{0:T(1024)S(1)}, ...), condition=%wide.region_5.6_spmd.clone, body=%wide.region_3.5_spmd.clone.sunk | while | flops 1582083 | bytes 2154591 | solution.py:35
  26.5 0.3 maximum_reduce_fusion.6
  26.9 0.3 maximum_reduce_fusion.6
  28.4 7.0 %fusion.28 = (f32[1024]{0:T(1024)S(1)}, f32[512,1024]{1,0:T(8,128)S(1)}, f32[1024,512]{0,1:T(8,128)}) fusion(f32[512,1024]{1,0:T(8,128)S(1)} %get-tuple-element.314, f32[1024]{0:T(1024)S(1)} %divide_add_fusion.1, f32[512,512]{1,0:T(8,128)S(1)} %copy-done, f32[512,1024]{1,0:T(8,128)} %copy-done.4), kind=kOutput, calls=%fused_computation.53 | convolution fusion | flops 3226991616 | bytes 9445376 | tf_op jit(solution)/shard_map/dot_general | solution.py:60
  35.5 0.3 maximum_reduce_fusion.2
  35.8 0.9 copy-done.1
  36.8 11.3 %while.35 = (s32[]{:T(128)}, f32[1024]{0:T(1024)S(1)}, f32[1024]{0:T(1024)S(1)}, f32[1024]{0:T(1024)S(1)}, f32[1024]{0:T(1024)S(1)}, /*index=5*/f32[512,1024]{1,0:T(8,128)}, s32[]{:T(128)}, s32[]{:T(128)}) while((s32[]{:T(128)}, f32[1024]{0:T(1024)S(1)}, f32[1024]{0:T(1024)S(1)}, f32[1024]{0:T(1024)S(1)}, f32[1024]{0:T(1024)S(1)}, ...), condition=%wide.region_11.12_spmd.clone, body=%wide.region_9.0_spmd.clone.sunk | while | flops 1582083 | bytes 2154591 | solution.py:35
  36.8 1.8 %maximum_reduce_fusion.7 = f32[1024]{0:T(1024)S(1)} fusion(f32[512,1024]{1,0:T(8,128)} %get-tuple-element.311, f32[1024]{0:T(1024)S(1)} %add_multiply_fusion.7), kind=kLoop, calls=%fused_computation.7.clone.1 | loop fusion | flops 1571840 | bytes 2105344 | tf_op jit(solution)/shard_map/while/body/eval_jaxpr/reduce_sum | solution.py:18
  38.7 1.8 %maximum_reduce_fusion.7 = f32[1024]{0:T(1024)S(1)} fusion(f32[512,1024]{1,0:T(8,128)} %get-tuple-element.311, f32[1024]{0:T(1024)S(1)} %add_multiply_fusion.7), kind=kLoop, calls=%fused_computation.7.clone.1 | loop fusion | flops 1571840 | bytes 2105344 | tf_op jit(solution)/shard_map/while/body/eval_jaxpr/reduce_sum | solution.py:18
  40.5 1.8 %maximum_reduce_fusion.7 = f32[1024]{0:T(1024)S(1)} fusion(f32[512,1024]{1,0:T(8,128)} %get-tuple-element.311, f32[1024]{0:T(1024)S(1)} %add_multiply_fusion.7), kind=kLoop, calls=%fused_computation.7.clone.1 | loop fusion | flops 1571840 | bytes 2105344 | tf_op jit(solution)/shard_map/while/body/eval_jaxpr/reduce_sum | solution.py:18
  42.4 1.8 %maximum_reduce_fusion.7 = f32[1024]{0:T(1024)S(1)} fusion(f32[512,1024]{1,0:T(8,128)} %get-tuple-element.311, f32[1024]{0:T(1024)S(1)} %add_multiply_fusion.7), kind=kLoop, calls=%fused_computation.7.clone.1 | loop fusion | flops 1571840 | bytes 2105344 | tf_op jit(solution)/shard_map/while/body/eval_jaxpr/reduce_sum | solution.py:18
  44.3 1.8 %maximum_reduce_fusion.7 = f32[1024]{0:T(1024)S(1)} fusion(f32[512,1024]{1,0:T(8,128)} %get-tuple-element.311, f32[1024]{0:T(1024)S(1)} %add_multiply_fusion.7), kind=kLoop, calls=%fused_computation.7.clone.1 | loop fusion | flops 1571840 | bytes 2105344 | tf_op jit(solution)/shard_map/while/body/eval_jaxpr/reduce_sum | solution.py:18
  46.2 1.8 %maximum_reduce_fusion.7 = f32[1024]{0:T(1024)S(1)} fusion(f32[512,1024]{1,0:T(8,128)} %get-tuple-element.311, f32[1024]{0:T(1024)S(1)} %add_multiply_fusion.7), kind=kLoop, calls=%fused_computation.7.clone.1 | loop fusion | flops 1571840 | bytes 2105344 | tf_op jit(solution)/shard_map/while/body/eval_jaxpr/reduce_sum | solution.py:18
  48.1 5.6 %fusion.9 = (f32[]{:T(128)}, f32[]{:T(128)}, f32[]{:T(128)}, f32[]{:T(128)}, f32[512,1024]{1,0:T(8,128)S(1)}) fusion(f32[1024,512]{0,1:T(8,128)} %get-tuple-element.172, f32[512,1024]{1,0:T(8,128)S(1)} %get-tuple-element.314, f32[1024]{0:T(1024)S(1)} %divide_add_fusion.1, f32[512,1024]{1,0:T(8,128)} %param.12, f32[1024,512]{0,1:T(8,128)} %get-tuple-element.173, ...), kind=kLoop, calls=%fused_computation.21 | loop fusion | flops 8388604 | bytes 12591120 | tf_op jit(solution)/shard_map/reduce_sum | solution.py:67
  53.7 2.0 %sub.115 = f32[512,1024]{1,0:T(8,128)} subtract(f32[512,1024]{1,0:T(8,128)S(1)} %copy-done.2, f32[512,1024]{1,0:T(8,128)S(1)} %get-tuple-element.159) | non-fusion elementwise | flops 524288 | bytes 6291456 | tf_op jit(solution)/shard_map/sub | solution.py:66
  55.7 40.5 %all-reduce = (f32[1]{0:T(128)}, f32[1]{0:T(128)}, f32[1]{0:T(128)}, f32[1]{0:T(128)}) all-reduce(f32[1]{0:T(128)} %bitcast.8, f32[1]{0:T(128)} %bitcast.7, f32[1]{0:T(128)} %bitcast.5, f32[1]{0:T(128)} %bitcast.4), channel_id=1, replica_groups=mesh['pix'=8,'band'=4] {'pix','band'}, use_global_device_ids=true, to_apply=%region_19.20 | all-reduce | flops 4 | bytes 32 | tf_op jit(solution)/shard_map/psum | solution.py:69
  96.2 2.6 %maximum_bitcast_fusion = (f32[1,2]{1,0:T(1,128)S(1)}, f32[1,2]{1,0:T(1,128)S(1)}) fusion(f32[1]{0:T(128)} %get-tuple-element.157, f32[1]{0:T(128)} %get-tuple-element.158, f32[1]{0:T(128)} %get-tuple-element.155, f32[1]{0:T(128)} %get-tuple-element.156), kind=kLoop, calls=%fused_computation.48 | loop fusion | flops 4 | bytes 32 | tf_op jit(solution)/shard_map/stack | solution.py:73
  98.8 0.6 fusion.24
  (44 shorter events, 1.3 us)
Async XLA Ops:
  0.6 16.8 %copy-start = (f32[512,512]{1,0:T(8,128)S(1)}, f32[512,512]{1,0:T(8,128)}, u32[]{:S(2)}) copy-start(f32[512,512]{1,0:T(8,128)} %param.11) | copy-start | bytes 3145732
  2.5 14.4 %all-to-all-start = ((bf16[56,4,1024]{2,0,1:T(8,128)(2,1)}), bf16[56,4,1024]{2,0,1:T(8,128)(2,1)S(1)}, u32[]{:S(2)}, u32[]{:S(2)}) async-start(bf16[56,4,1024]{2,0,1:T(8,128)(2,1)} %bitcast.34), calls=%async_computation | async-start | bytes 917504 | tf_op jit(solution)/shard_map/all_to_all | solution.py:50
  17.5 8.7 %copy-start.4 = (f32[512,1024]{1,0:T(8,128)}, f32[512,1024]{1,0:T(8,128)S(1)}, u32[]{:S(2)}) copy-start(f32[512,1024]{1,0:T(8,128)S(1)} %fusion.30) | copy-start | bytes 6291460
  35.5 1.3 %copy-start.1 = (f32[512,1024]{1,0:T(8,128)}, f32[512,1024]{1,0:T(8,128)S(1)}, u32[]{:S(2)}) copy-start(f32[512,1024]{1,0:T(8,128)S(1)} %get-tuple-element.295) | copy-start | bytes 6291460
  48.1 5.6 %copy-start.2 = (f32[512,1024]{1,0:T(8,128)S(1)}, f32[512,1024]{1,0:T(8,128)}, u32[]{:S(2)}) copy-start(f32[512,1024]{1,0:T(8,128)} %get-tuple-element.315) | copy-start | bytes 6291460
  53.7 2.0 %copy-start.3 = (f32[512,1024]{1,0:T(8,128)}, f32[512,1024]{1,0:T(8,128)S(1)}, u32[]{:S(2)}) copy-start(f32[512,1024]{1,0:T(8,128)S(1)} %get-tuple-element.159) | copy-start | bytes 6291460
where the time goes:
time: 99.9 us; the launch traced here: 99.4 us
  blocking collectives  50.7 us (51%)
  other arithmetic  24.3 us (24%)
  matrix products  16.2 us (16%)
  starting transfers between devices  4.26 us (4%)
  local copies, waits for them, and re-layouts  2.88 us (3%)
    psum x1, blocking collectives, body(): primal_sum, change_sum = lax.psum((primal_sum, change_sum), ('pix', 'band'))  40.5 us
    dot_general x2, matrix products, body(): jnp.dot(gram_inverse, fit_term / penalty + current - scaled_dual, precisi...  15.7 us
    reduce_sum x14, other arithmetic, mass_at(): return jnp.sum(jnp.maximum(shifted - level[None, :], 0.0), axis=0)  13.3 us
    all_gather x1, blocking collectives, body(): all_rows = lax.all_gather(endmembers, 'band', axis=0, tiled=True)  10.2 us
    reduce_sum x1, other arithmetic, body(): primal_sum = jnp.sum((primal - updated) ** 2)  5.61 us
    all_to_all x1, starting transfers between devices, body(): lax.all_to_all(spectra, 'band', split_axis=1, concat_axis=0, tiled=True)  4.26 us
    another operation x1, other arithmetic, body(): totals = jnp.stack([jnp.stack(primal_list), jnp.stack(change_list)])  2.6 us
    sub x1, other arithmetic, body(): scaled_dual = scaled_dual + primal - updated  2 us
  transfers between devices with their start and end apart: 1, of which 0 were waited for; matrix products, arithmetic and copies ran while one was open for 0% of the time, Pallas kernels for 0%

commit v1 on v0

--- a/solution.py
+++ b/solution.py
@@ -2,6 +2,7 @@
 import jax.numpy as jnp
 from jax import lax
 from jax.sharding import PartitionSpec as P
+from jax.lax import all_to_all, axis_size
 
 B = 224
 K = 512
@@ -47,7 +48,20 @@
 
 def body(spectra, endmembers, gram_inverse, abundances, duals):
     penalty = B / (2.0 * K * K)
-    exchanged = lax.all_to_all(spectra, "band", split_axis=1, concat_axis=0, tiled=True)
+
+    def _mix_sites(dimension_no, inp, d_out=0):
+        odd = jnp.concatenate(
+            all_to_all(
+                jnp.stack(jnp.split(inp, axis_size("band"), axis=dimension_no)),
+                split_axis=0,
+                concat_axis=0,
+                axis_name="band",
+            ),
+            axis=d_out,
+        )
+        return odd
+
+    exchanged = _mix_sites(1, spectra)
     all_rows = lax.all_gather(endmembers, "band", axis=0, tiled=True)
     fit_term = contract_bands(all_rows, exchanged)
     fit_term = fit_term / K

time: 99.9 us -> 104 us (1.041)
  local copies, waits for them, and re-layouts: 2.88 us -> 15.4 us
  other arithmetic: 24.3 us -> 18.3 us
  blocking collectives: 50.7 us -> 48.3 us
    unnamed x10 -> x16, local copies, waits for them, and re-layouts: 0.98 us -> 14.2 us
    reduce_sum x14, other arithmetic: 13.3 us -> 7.65 us  [mass_at(): return jnp.sum(jnp.maximum(shifted - level[None, :], 0.0), axis=0)]
    all_gather x1, blocking collectives: 10.2 us -> 6.93 us  [body(): all_rows = lax.all_gather(endmembers, 'band', axis=0, tiled=True)]
    sub x1 -> x0, other arithmetic: 2 us -> none  [body(): scaled_dual = scaled_dual + primal - updated]
    all_to_all x1 -> x0, local copies, waits for them, and re-layouts: 1.9 us -> none  [body(): lax.all_to_all(spectra, 'band', split_axis=1, concat_axis=0, tiled=True)]
    dot_general x2, matrix products: 15.7 us -> 14.1 us  [body(): jnp.dot(gram_inverse, fit_term / penalty + current - scaled_dual, precisi...]
    another operation x0 -> x1, local copies, waits for them, and re-layouts: none -> 1.19 us  [_mix_sites(): jnp.stack(jnp.split(inp, axis_size('band'), axis=dimension_no))]
    dot_general x1, matrix products: 0.47 us -> 1.64 us  [contract_bands(): lax.dot_general(signatures, columns, (((0,), (0,)), ((), ())), preferred_...]
  transfers between devices with their start and end apart: 1 -> 1, of which waited for: 0 -> 0; matrix products, arithmetic and copies ran while one was open for 0% -> 5% of each run, Pallas kernels for 0% -> 0%
where the time goes in v1:
time: 104 us; the launch traced here: 103 us
  blocking collectives  48.3 us (46%)
  other arithmetic  18.3 us (18%)
  matrix products  15.7 us (15%)
  local copies, waits for them, and re-layouts  15.4 us (15%)
  starting transfers between devices  4.26 us (4%)
    psum x1, blocking collectives, body(): primal_sum, change_sum = lax.psum((primal_sum, change_sum), ('pix', 'band'))  41.4 us
    unnamed x16, local copies, waits for them, and re-layouts  14.2 us
    dot_general x2, matrix products, body(): jnp.dot(gram_inverse, fit_term / penalty + current - scaled_dual, precisi...  14.1 us
    reduce_sum x14, other arithmetic, mass_at(): return jnp.sum(jnp.maximum(shifted - level[None, :], 0.0), axis=0)  7.65 us
    all_gather x1, blocking collectives, body(): all_rows = lax.all_gather(endmembers, 'band', axis=0, tiled=True)  6.93 us
    reduce_sum x1, other arithmetic, body(): primal_sum = jnp.sum((primal - updated) ** 2)  6.42 us
    all_to_all x1, starting transfers between devices, _mix_sites(): all_to_all(jnp.stack(jnp.split(inp, axis_size('band'), axis=dimension_no)...  4.26 us
    another operation x1, other arithmetic, body(): totals = jnp.stack([jnp.stack(primal_list), jnp.stack(change_list)])  2.6 us
  transfers between devices with their start and end apart: 1, of which 0 were waited for; matrix products, arithmetic and copies ran while one was open for 5% of the time, Pallas kernels for 0%

profile of v1, /device:TPU:0, one launch (start us, length us, event | category | flops | bytes accessed | tf_op | source)
XLA Modules:
  0.0 103.1 jit_solution(4919223918417186719)
XLA Ops:
  0.6 1.2 %slice_bitcast_fusion.3 = (bf16[1,56,1024]{2,1,0:T(8,128)(2,1)S(1)}, bf16[1,56,1024]{2,1,0:T(8,128)(2,1)S(1)}, bf16[1,56,1024]{2,1,0:T(8,128)(2,1)S(1)}, bf16[1,56,1024]{2,1,0:T(8,128)(2,1)S(1)}) fusion(bf16[56,4096]{1,0:T(8,128)(2,1)} %param.9), kind=kLoop, calls=%fused_computation.45 | loop fusion | bytes 917504 | tf_op jit(solution)/shard_map/stack | solution.py:55
  1.8 0.8 pad_maximum_fusion
  2.7 4.3 %all-to-all-start = ((bf16[4,56,1024]{2,1,0:T(8,128)(2,1)}), bf16[4,56,1024]{2,1,0:T(8,128)(2,1)}, u32[]{:S(2)}, u32[]{:S(2)}) async-start(bf16[4,56,1024]{2,1,0:T(8,128)(2,1)} %pad_maximum_fusion), calls=%async_computation | async-start | bytes 917504 | tf_op jit(solution)/shard_map/all_to_all | solution.py:54
  6.9 1.9 %copy.8 = f32[512,1024]{0,1:T(8,128)S(1)} copy(f32[512,1024]{1,0:T(8,128)} %param.12) | data formatting | bytes 4194304 | tf_op args[3]
  8.9 3.7 %copy.9 = f32[512,1024]{0,1:T(8,128)} copy(f32[512,1024]{1,0:T(8,128)} %param.13) | data formatting | bytes 4194304 | tf_op args[4]
  12.5 6.9 %all_gather.3 = bf16[224,512]{1,0:T(8,128)(2,1)S(1)} all-gather(bf16[56,512]{1,0:T(8,128)(2,1)S(1)} %copy-done.4), channel_id=1, replica_groups=mesh['pix'=8,'band'=4] {'band'}, dimensions={0}, use_global_device_ids=true | all-gather | bytes 286720 | tf_op jit(solution)/shard_map/all_gather | solution.py:65
  19.5 1.6 %fusion.31 = f32[1024,512]{1,0:T(8,128)S(1)} fusion(bf16[224,1024]{1,0:T(8,128)(2,1)} %bitcast.4, bf16[224,512]{1,0:T(8,128)(2,1)S(1)} %all_gather.3), kind=kOutput, calls=%fused_computation.60 | convolution fusion | flops 234881024 | bytes 2785280 | tf_op jit(solution)/shard_map/dot_general | solution.py:44
  21.2 5.2 %fusion.30 = (f32[1024]{0:T(1024)S(1)}, f32[512,1024]{0,1:T(8,128)}, f32[1024,512]{1,0:T(8,128)}) fusion(f32[512,1024]{0,1:T(8,128)S(1)} %copy-done.3, f32[512,512]{1,0:T(8,128)S(1)} %copy-done, f32[512,1024]{0,1:T(8,128)S(1)} %copy.8, f32[1024,512]{1,0:T(8,128)S(1)} %fusion.31), kind=kOutput, calls=%fused_computation.59 | convolution fusion | flops 3223845888 | bytes 11538432 | tf_op jit(solution)/shard_map/dot_general | solution.py:74
  26.5 1.9 %copy.12 = f32[512,1024]{1,0:T(8,128)S(1)} copy(f32[512,1024]{0,1:T(8,128)} %get-tuple-element.177) | data formatting | bytes 4194304
  28.4 2.2 %maximum_reduce_fusion.3 = (f32[1024]{0:T(1024)S(1)}, f32[1024]{0:T(1024)S(1)}) fusion(f32[512,1024]{0,1:T(8,128)} %get-tuple-element.177, f32[1024]{0:T(1024)S(1)} %add_multiply_fusion.3), kind=kLoop, calls=%fused_computation.34 | loop fusion | flops 2095104 | bytes 2109440 | tf_op jit(solution)/shard_map/reduce_sum | solution.py:19
  30.6 1.9 %while.34 = (s32[]{:T(128)}, f32[1024]{0:T(1024)S(1)}, f32[1024]{0:T(1024)S(1)}, f32[1024]{0:T(1024)S(1)}, f32[1024]{0:T(1024)S(1)}, /*index=5*/f32[512,1024]{1,0:T(8,128)S(1)}, s32[]{:T(128)}, s32[]{:T(128)}) while((s32[]{:T(128)}, f32[1024]{0:T(1024)S(1)}, f32[1024]{0:T(1024)S(1)}, f32[1024]{0:T(1024)S(1)}, f32[1024]{0:T(1024)S(1)}, ...), condition=%wide.region_5.6_spmd.clone, body=%wide.region_3.5_spmd.clone.sunk | while | flops 1582083 | bytes 2154591 | solution.py:36
  30.6 0.3 maximum_reduce_fusion.6
  32.2 0.3 maximum_reduce_fusion.6
  32.5 8.9 %fusion.29 = (f32[1024]{0:T(1024)S(1)}, f32[512,1024]{0,1:T(8,128)}, f32[1024,512]{1,0:T(8,128)}) fusion(f32[512,1024]{0,1:T(8,128)} %get-tuple-element.177, f32[1024]{0:T(1024)S(1)} %divide_add_fusion.1, f32[512,512]{1,0:T(8,128)S(1)} %copy-done, f32[1024,512]{1,0:T(8,128)} %copy-done.2), kind=kOutput, calls=%fused_computation.58 | convolution fusion | flops 3226991616 | bytes 9445376 | tf_op jit(solution)/shard_map/dot_general | solution.py:74
  41.3 1.9 %copy.14 = f32[512,1024]{1,0:T(8,128)S(1)} copy(f32[512,1024]{0,1:T(8,128)} %get-tuple-element.175) | data formatting | bytes 4194304
  43.3 2.2 %maximum_reduce_fusion.2 = (f32[1024]{0:T(1024)S(1)}, f32[1024]{0:T(1024)S(1)}) fusion(f32[512,1024]{0,1:T(8,128)} %get-tuple-element.175, f32[1024]{0:T(1024)S(1)} %add_multiply_fusion.2), kind=kLoop, calls=%fused_computation.31 | loop fusion | flops 2095104 | bytes 2109440 | tf_op jit(solution)/shard_map/reduce_sum | solution.py:19
  45.4 1.9 %while.35 = (s32[]{:T(128)}, f32[1024]{0:T(1024)S(1)}, f32[1024]{0:T(1024)S(1)}, f32[1024]{0:T(1024)S(1)}, f32[1024]{0:T(1024)S(1)}, /*index=5*/f32[512,1024]{1,0:T(8,128)S(1)}, s32[]{:T(128)}, s32[]{:T(128)}) while((s32[]{:T(128)}, f32[1024]{0:T(1024)S(1)}, f32[1024]{0:T(1024)S(1)}, f32[1024]{0:T(1024)S(1)}, ...), condition=%wide.region_11.12_spmd.clone, body=%wide.region_9.0_spmd.clone.sunk | while | flops 1582083 | bytes 2154591 | solution.py:36
  45.8 0.3 maximum_reduce_fusion.7
  47.4 6.4 %fusion.9 = (f32[]{:T(128)}, f32[]{:T(128)}, f32[]{:T(128)}, f32[]{:T(128)}, f32[512,1024]{0,1:T(8,128)}, /*index=5*/f32[512,1024]{0,1:T(8,128)S(1)}) fusion(f32[1024,512]{1,0:T(8,128)} %get-tuple-element.192, f32[512,1024]{0,1:T(8,128)} %get-tuple-element.177, f32[1024]{0:T(1024)S(1)} %divide_add_fusion.1, f32[512,1024]{0,1:T(8,128)} %copy-done.1, ...), kind=kLoop, calls=%fused_computation.21 | loop fusion | flops 8912892 | bytes 14688272 | tf_op jit(solution)/shard_map/reduce_sum | solution.py:81
  53.8 2.9 %copy.16 = f32[512,1024]{1,0:T(8,128)} copy(f32[512,1024]{0,1:T(8,128)} %get-tuple-element.186) | data formatting | bytes 4194304
  56.7 1.8 %copy.17 = f32[512,1024]{1,0:T(8,128)} copy(f32[512,1024]{0,1:T(8,128)S(1)} %get-tuple-element.187) | data formatting | bytes 4194304
  58.5 41.4 %all-reduce = (f32[1]{0:T(128)}, f32[1]{0:T(128)}, f32[1]{0:T(128)}, f32[1]{0:T(128)}) all-reduce(f32[1]{0:T(128)} %bitcast.12, f32[1]{0:T(128)} %bitcast.11, f32[1]{0:T(128)} %bitcast.9, f32[1]{0:T(128)} %bitcast.8), channel_id=1, replica_groups=mesh['pix'=8,'band'=4] {'pix','band'}, use_global_device_ids=true, to_apply=%region_19.20 | all-reduce | flops 4 | bytes 32 | tf_op jit(solution)/shard_map/psum | solution.py:83
  99.9 2.6 %maximum_bitcast_fusion = (f32[1,2]{1,0:T(1,128)S(1)}, f32[1,2]{1,0:T(1,128)S(1)}) fusion(f32[1]{0:T(128)} %get-tuple-element.172, f32[1]{0:T(128)} %get-tuple-element.173, f32[1]{0:T(128)} %get-tuple-element.170, f32[1]{0:T(128)} %get-tuple-element.171), kind=kLoop, calls=%fused_computation.52 | loop fusion | flops 4 | bytes 32 | tf_op jit(solution)/shard_map/stack | solution.py:87
  102.5 0.6 fusion.24
  (50 shorter events, 2.8 us)
Async XLA Ops:
  0.6 20.5 %copy-start = (f32[512,512]{1,0:T(8,128)S(1)}, f32[512,512]{1,0:T(8,128)}, u32[]{:S(2)}) copy-start(f32[512,512]{1,0:T(8,128)} %param.11) | copy-start | bytes 3145732
  2.7 16.8 %all-to-all-start = ((bf16[4,56,1024]{2,1,0:T(8,128)(2,1)}), bf16[4,56,1024]{2,1,0:T(8,128)(2,1)}, u32[]{:S(2)}, u32[]{:S(2)}) async-start(bf16[4,56,1024]{2,1,0:T(8,128)(2,1)} %pad_maximum_fusion), calls=%async_computation | async-start | bytes 917504 | tf_op jit(solution)/shard_map/all_to_all | solution.py:54
  8.9 12.3 %copy-start.1 = (f32[512,1024]{0,1:T(8,128)}, f32[512,1024]{0,1:T(8,128)S(1)}, u32[]{:S(2)}) copy-start(f32[512,1024]{0,1:T(8,128)S(1)} %copy.8) | copy-start | bytes 6291460
  8.9 3.7 %copy-start.4 = (bf16[56,512]{1,0:T(8,128)(2,1)S(1)}, bf16[56,512]{1,0:T(8,128)(2,1)}, u32[]{:S(2)}) copy-start(bf16[56,512]{1,0:T(8,128)(2,1)} %param.10) | copy-start | bytes 172036
  19.5 1.7 %copy-start.3 = (f32[512,1024]{0,1:T(8,128)S(1)}, f32[512,1024]{0,1:T(8,128)}, u32[]{:S(2)}) copy-start(f32[512,1024]{0,1:T(8,128)} %copy.9) | copy-start | bytes 6291460
  21.2 5.2 %copy-start.2 = (f32[1024,512]{1,0:T(8,128)}, f32[1024,512]{1,0:T(8,128)S(1)}, u32[]{:S(2)}) copy-start(f32[1024,512]{1,0:T(8,128)S(1)} %fusion.31) | copy-start | bytes 6291460
